TPU v7x, 16 devices: a 4x2x1 block of a 4x4x8 slice. The times are simulated.
16 devices in a mesh: data: 2 (over y, z), expert: 8 (over x, core).
Axes of the slice: x: 4, y: 2, z: 1, core: 2. Of those that a mesh axis runs over, the one named last changes fastest.
The devices are a block of a 4x4x8 slice.
Arguments:
- token_rows: bfloat16 [2048, 2048], P(('data', 'expert')), parts along dimension 0
- expert_ids: int32 [2048, 6], P(('data', 'expert')), parts along dimension 0
- gate_weights: float32 [2048, 6], P(('data', 'expert')), parts along dimension 0
- w_in: bfloat16 [64, 2048, 1408], P('expert')
- w_out: bfloat16 [64, 1408, 2048], P('expert')
Outputs:
- output: bfloat16 [2048, 2048], P(('data', 'expert')), parts along dimension 0
There are 2 independent parts. A program takes and returns all parts, laid end to end along the dimension named above; an argument that names none is the same for every part.
All inputs are finite; a program needn't handle non-finite values.
Results may differ from a plain program's by a relative error of at most 0.001.
Values are sent between devices in bfloat16 or wider.
A program may use at most 768 MiB of HBM per device.

v0:
```python
import functools

import jax
import jax.numpy as jnp
from jax import lax
from jax.experimental import pallas as pl
from jax.experimental.pallas import tpu as pltpu
from jax.sharding import PartitionSpec as P

MESH = pl.DeviceIdType.MESH
F32 = jnp.float32
BF16 = jnp.bfloat16
AXIS = "expert"
LANES = 128
IN_BLOCKS = 8
IN_DEPTH = 3
OUT_COLS = 256
OUT_DEPTH = 2
AHEAD = 3
LAG = 3
VMEM_BYTES = 62 * 2 ** 20
GELU_A = 0.7978845608028654
GELU_B = 0.044715 * GELU_A
PICK_PARTS = 4
BEHIND = 1
PICK_COLS = 256
BIG_BF16 = 3.3895313892515355e38

OWN_R, OWN_L, OWN_P, RELAY_R, RELAY_L, FWD_L, FWD_R, FWD_A, FWD_B = range(9)
PART, FAR_R, FAR_L, NEAR_R, NEAR_L, MIX_R, MIX_L, PART_REST = range(8)


def gelu(x):
    half = 0.5 * x
    return half + half * jnp.tanh(x * (GELU_A + GELU_B * (x * x)))


def body(n, capacity, ids_hbm, gate_hbm, x_hbm, w_in, w_out, out_ref,
         ids_all, gates_all, x_all, pick, packed, mix, xg, acc, hid, spread, obuf0, obuf1,
         part_send, part_recv, total, far_recv, fin_recv, win_buf, wout_buf,
         meta_ssem, meta_rsem, d_ssem, d_rsem, r_ssem, r_rsem, p_rsem, x_sem, win_sem, wout_sem, own_sem):
    top_k, tokens = ids_hbm.shape
    local_e, model, hidden = w_in.shape
    chips = n // 2
    kc_n = model // IN_BLOCKS
    oc_n = model // OUT_COLS
    slots = local_e * capacity

    me = lax.axis_index(AXIS)
    core = lax.rem(me, 2)
    chip = me // 2
    buddy = me + 1 - 2 * core
    other = 1 - core
    c_right = lax.rem(chip + 1, chips)
    c_far = lax.rem(chip + 2, chips)
    c_left = lax.rem(chip + 3, chips)

    def dev(c, k):
        return 2 * c + k

    right = dev(c_right, core)
    left = dev(c_left, core)

    def alone(fn):
        pl.when(me >= 0)(fn)

    def win_copy(e, kc):
        slot = lax.rem(kc, IN_DEPTH)
        return pltpu.make_async_copy(
            w_in.at[e, pl.ds(kc * kc_n, kc_n), :], win_buf.at[slot, e], win_sem.at[slot])

    def win_wait(kc):
        slot = lax.rem(kc, IN_DEPTH)
        pltpu.make_async_copy(w_in.at[:, pl.ds(0, kc_n), :], win_buf.at[slot], win_sem.at[slot]).wait()

    def wout_copy(e, oc):
        slot = lax.rem(oc, OUT_DEPTH)
        return pltpu.make_async_copy(
            w_out.at[e, :, pl.ds(oc * OUT_COLS, OUT_COLS)], wout_buf.at[slot, e], wout_sem.at[slot])

    def wout_wait(oc):
        slot = lax.rem(oc, OUT_DEPTH)
        pltpu.make_async_copy(w_out.at[:, :, pl.ds(0, OUT_COLS)], wout_buf.at[slot], wout_sem.at[slot]).wait()

    def x_rows(kc, d):
        return x_all.at[kc, pl.ds(d * tokens, tokens), :]

    def x_half(kc, d, h):
        half = tokens // 2
        return x_all.at[kc, pl.ds(d * tokens + h * half, half), :]

    def x_copy(kc):
        return pltpu.make_async_copy(
            x_hbm.at[:, pl.ds(kc * kc_n, kc_n)], x_rows(kc, me), x_sem)

    barrier = pltpu.get_barrier_semaphore()
    for d in range(1, n):
        pl.semaphore_signal(barrier, inc=1, device_id={AXIS: lax.rem(me + d, n)}, device_id_type=MESH)

    own_meta = (
        pltpu.make_async_copy(ids_hbm, ids_all.at[me], own_sem.at[0]),
        pltpu.make_async_copy(gate_hbm, gates_all.at[me], own_sem.at[1]),
    )
    for c in own_meta:
        c.start()
    for kc in range(IN_BLOCKS):
        x_copy(kc).start()

    @pl.loop(0, IN_DEPTH)
    def _(kc):
        for e in range(local_e):
            win_copy(e, kc).start()

    @pl.loop(0, OUT_DEPTH)
    def _(oc):
        for e in range(local_e):
            wout_copy(e, oc).start()

    with jax.named_scope("barrier"):
        pl.semaphore_wait(barrier, n - 1)
        for c in own_meta:
            c.wait()

    def meta_copies(d):
        to = lax.rem(me + d, n)
        return (
            pltpu.make_async_remote_copy(
                src_ref=ids_all.at[me], dst_ref=ids_all.at[me], send_sem=meta_ssem.at[0], recv_sem=meta_rsem.at[0],
                device_id={AXIS: to}, device_id_type=MESH),
            pltpu.make_async_remote_copy(
                src_ref=gates_all.at[me], dst_ref=gates_all.at[me], send_sem=meta_ssem.at[1], recv_sem=meta_rsem.at[1],
                device_id={AXIS: to}, device_id_type=MESH),
        )

    def meta_all():
        ids_part, gates_part = ids_all.at[pl.ds(0, n - 1)], gates_all.at[pl.ds(0, n - 1)]
        return (
            pltpu.make_async_remote_copy(
                src_ref=ids_part, dst_ref=ids_part, send_sem=meta_ssem.at[0], recv_sem=meta_rsem.at[0],
                device_id={AXIS: buddy}, device_id_type=MESH),
            pltpu.make_async_remote_copy(
                src_ref=gates_part, dst_ref=gates_part, send_sem=meta_ssem.at[1], recv_sem=meta_rsem.at[1],
                device_id={AXIS: buddy}, device_id_type=MESH),
        )

    for d in range(1, n):
        for c in meta_copies(d):
            c.start()

    def dcopy(kind, kc, ref, to):
        group = 0 if kind in (OWN_R, OWN_L) else 1 if kind in (RELAY_R, RELAY_L) else 2
        return pltpu.make_async_remote_copy(
            src_ref=ref, dst_ref=ref, send_sem=d_ssem, recv_sem=d_rsem.at[group, kc],
            device_id={AXIS: to}, device_id_type=MESH)

    def d_wait(kind, kc, rows):
        dcopy(kind, kc, x_all.at[kc, pl.ds(0, rows), :], buddy).wait_recv()

    def d_flush():
        sent = x_all.at[:, pl.ds(0, 7 * tokens), :]
        dcopy(OWN_R, 0, sent, buddy).wait_send()

    far = dev(c_far, core)

    def d_sent(kind, kc):
        if kind == OWN_R:
            return dcopy(kind, kc, x_rows(kc, me), right)
        if kind == OWN_L:
            return dcopy(kind, kc, x_rows(kc, me), left)
        if kind == OWN_P:
            return dcopy(kind, kc, x_rows(kc, me), buddy)
        if kind == RELAY_R:
            return dcopy(kind, kc, x_half(kc, left, 0), right)
        if kind == RELAY_L:
            return dcopy(kind, kc, x_half(kc, right, 1), left)
        if kind == FWD_L:
            return dcopy(kind, kc, x_rows(kc, left), buddy)
        if kind == FWD_R:
            return dcopy(kind, kc, x_rows(kc, right), buddy)
        if kind == FWD_A:
            return dcopy(kind, kc, x_half(kc, far, 0), buddy)
        return dcopy(kind, kc, x_half(kc, far, 1), buddy)

    def send_own(kc):
        for kind in (OWN_R, OWN_L, OWN_P):
            d_sent(kind, kc).start()

    def stage1(kc):
        d_wait(OWN_R, kc, 2 * tokens)
        for kind in (RELAY_R, RELAY_L, FWD_L, FWD_R):
            d_sent(kind, kc).start()

    def stage2(kc):
        d_wait(RELAY_R, kc, tokens)
        for kind in (FWD_A, FWD_B):
            d_sent(kind, kc).start()

    def stage3(kc):
        d_wait(OWN_P, kc, chips * tokens)

    with jax.named_scope("own"):
        mine = x_all.at[:, pl.ds(me * tokens, tokens), :]
        pltpu.make_async_copy(mine, mine, x_sem).wait()
        for kc in range(AHEAD):
            send_own(kc)

    with jax.named_scope("meta_wait"):
        for c in meta_all():
            c.wait_recv()

    sub = lax.broadcasted_iota(jnp.int32, (local_e, tokens), 0) + me * local_e
    hit = {}
    for b in range(n):
        for j in range(top_k):
            hit[b, j] = jnp.where(ids_all[b, j:j + 1, :] == sub, 1.0, 0.0).astype(F32)
    hits = jnp.concatenate([hit[b, j] for b in range(n) for j in range(top_k)], axis=0).astype(BF16)
    t_from = lax.broadcasted_iota(jnp.int32, (tokens, tokens), 0)
    t_to = lax.broadcasted_iota(jnp.int32, (tokens, tokens), 1)
    earlier = jnp.where(t_from < t_to, 1.0, 0.0).astype(BF16)
    ones = jnp.full((tokens, tokens), 1.0, BF16)
    within = jnp.dot(hits, earlier, preferred_element_type=F32)
    sums = jnp.dot(hits, ones, preferred_element_type=F32)
    running = jnp.zeros((local_e, tokens), F32)
    rank = [jnp.zeros((local_e, tokens), F32) for _ in range(n)]
    for j in range(top_k):
        for b in range(n):
            at = (b * top_k + j) * local_e
            rank[b] = rank[b] + hit[b, j] * (running + within[at:at + local_e])
            running = running + sums[at:at + local_e]
    slot_row = lax.broadcasted_iota(jnp.int32, (capacity, tokens), 0).astype(F32)
    for b in range(n):
        has = jnp.zeros((local_e, tokens), F32)
        gate = jnp.zeros((local_e, tokens), F32)
        for j in range(top_k):
            has = has + hit[b, j]
            gate = gate + hit[b, j] * gates_all[b, j:j + 1, :]
        slot = jnp.where((has > 0.0) & (rank[b] < capacity), rank[b], -1.0)
        g1 = jnp.minimum(gate, BIG_BF16).astype(BF16).astype(F32)
        g2 = (gate - g1).astype(BF16).astype(F32)
        g3 = gate - g1 - g2
        packed[b] = jnp.concatenate([slot, g1, g2, g3], axis=0)
        for e in range(local_e):
            at = b * tokens % PICK_COLS
            pick[b * tokens // PICK_COLS, e * capacity:(e + 1) * capacity, at:at + tokens] = jnp.where(
                slot[e:e + 1, :] == slot_row, 1.0, 0.0).astype(BF16)

    acc[...] = jnp.zeros_like(acc)

    part_c = 2 * LANES
    for q in range(4):
        at = lax.broadcasted_iota(jnp.int32, (LANES, slots), 1)
        row = lax.broadcasted_iota(jnp.int32, (LANES, slots), 0) - q * local_e
        spread[:, q * slots:(q + 1) * slots] = jnp.where(
            (at >= row * capacity) & (at < (row + 1) * capacity) & (row >= 0) & (row < local_e), 1.0, 0.0).astype(BF16)

    def mix_rows(b):
        row = pl.multiple_of((lax.rem(b, 2) * chips + b // 2) * tokens, tokens)
        cols = jnp.concatenate(
            [packed[b], jnp.zeros((LANES - 4 * local_e, tokens), F32)], axis=0).T.astype(BF16)
        for p in range(slots // part_c):
            at = lax.broadcasted_iota(jnp.int32, (1, part_c), 1) + p * part_c
            rel = at
            for e in range(1, local_e):
                rel = jnp.where(at >= e * capacity, at - e * capacity, rel)
            rel = rel.astype(F32)

            def repeat(q):
                return jnp.dot(cols, spread[:, q * slots + p * part_c:q * slots + (p + 1) * part_c],
                               preferred_element_type=F32)

            slot_at = repeat(0)
            for k in range(3):
                mix[k, pl.ds(row, tokens), p * part_c:(p + 1) * part_c] = jnp.where(
                    slot_at == rel, repeat(k + 1), 0.0).astype(BF16)

    def mix_range(lo, hi):
        with jax.named_scope("mix"):
            pl.loop(lo, hi)(mix_rows)

    with jax.named_scope("s1"):
        stage1(0)
        send_own(AHEAD)
    mix_range(0, n // 2)
    with jax.named_scope("s1"):
        stage1(1)
        send_own(AHEAD + 1)
    with jax.named_scope("s2"):
        stage2(0)

    pick_rows = slots // PICK_PARTS

    def gather(kc):
        for i in range(PICK_PARTS):
            val = None
            for p in range(n * tokens // PICK_COLS):
                term = jnp.dot(pick[p, i * pick_rows:(i + 1) * pick_rows, :],
                               x_all[kc, p * PICK_COLS:(p + 1) * PICK_COLS, :], preferred_element_type=F32)
                val = term if val is None else val + term
            xg[i * pick_rows // capacity:(i + 1) * pick_rows // capacity] = val.astype(BF16).reshape(
                pick_rows // capacity, capacity, kc_n)

    with jax.named_scope("s1"):
        stage1(2)
        send_own(AHEAD + 2)
    mix_range(n // 2, n)

    @pl.loop(0, IN_BLOCKS - 1)
    def _(kc):
        with jax.named_scope("s1"):
            @pl.when(kc + 3 < IN_BLOCKS)
            def _():
                stage1(kc + 3)

            @pl.when(kc + 3 + AHEAD < IN_BLOCKS)
            def _():
                send_own(kc + 3 + AHEAD)

        with jax.named_scope("s2"):
            stage2(kc + 1)
        with jax.named_scope("s3"):
            stage3(kc)

        with jax.named_scope("up"):
            win_wait(kc)

            @alone
            def _():
                gather(kc)
                for e in range(local_e):
                    acc[e] = acc[e] + jnp.dot(xg[e], win_buf[lax.rem(kc, IN_DEPTH), e], preferred_element_type=F32)

            @pl.when(kc + IN_DEPTH < IN_BLOCKS)
            def _():
                for e in range(local_e):
                    win_copy(e, kc + IN_DEPTH).start()

    last = IN_BLOCKS - 1
    with jax.named_scope("s3"):
        stage3(last)
    def rcopy(kind, oc, src, dst, to):
        ssem = r_ssem.at[lax.rem(oc, 2)] if kind in (PART, PART_REST) else r_ssem.at[2]
        if kind in (PART, PART_REST):
            rsem = p_rsem.at[int(kind == PART_REST), lax.rem(oc, 2)]
        else:
            rsem = r_rsem.at[int(kind not in (FAR_R, FAR_L)), oc]
        return pltpu.make_async_remote_copy(
            src_ref=src, dst_ref=dst, send_sem=ssem, recv_sem=rsem,
            device_id={AXIS: to}, device_id_type=MESH)

    def r_copy(kind, oc):
        if kind == PART:
            return rcopy(kind, oc, part_send.at[lax.rem(oc, 2), c_far], part_recv.at[oc, c_far], buddy)
        if kind == FAR_R:
            return rcopy(kind, oc, total.at[oc, c_far, 0], far_recv.at[oc, 0], right)
        if kind == FAR_L:
            return rcopy(kind, oc, total.at[oc, c_far, 1], far_recv.at[oc, 1], left)
        if kind == NEAR_R:
            return rcopy(kind, oc, total.at[oc, c_right, 1], fin_recv.at[oc, 0, 1], right)
        if kind == NEAR_L:
            return rcopy(kind, oc, total.at[oc, c_left, 0], fin_recv.at[oc, 1, 0], left)
        if kind == MIX_R:
            return rcopy(kind, oc, total.at[oc, c_right, 0], fin_recv.at[oc, 0, 0], right)
        return rcopy(kind, oc, total.at[oc, c_left, 1], fin_recv.at[oc, 1, 1], left)

    rows = chips * tokens
    half = OUT_COLS // 2

    def partial_of(rail, t, obuf, dst):
        at = pl.multiple_of(rail * rows + t * tokens, tokens)
        val = jnp.dot(mix[0, pl.ds(at, tokens), :], obuf[...], preferred_element_type=F32)
        val += jnp.dot(mix[1, pl.ds(at, tokens), :], obuf[...], preferred_element_type=F32)
        val += jnp.dot(mix[2, pl.ds(at, tokens), :], obuf[...], preferred_element_type=F32)
        for h in range(2):
            dst[t, h] = val[:, h * half:(h + 1) * half]

    def finish_far(oc):
        rcopy(FAR_R, oc, far_recv.at[oc], far_recv.at[oc], buddy).wait_recv()
        total[oc, c_right, 0] = total[oc, c_right, 0] + far_recv[oc, 0]
        r_copy(MIX_R, oc).start()
        total[oc, c_left, 1] = total[oc, c_left, 1] + far_recv[oc, 1]
        r_copy(MIX_L, oc).start()

    per_in = kc_n // OUT_COLS

    def finish(oc):
        rcopy(NEAR_R, oc, fin_recv.at[oc], fin_recv.at[oc], buddy).wait_recv()
        for h in range(2):
            at = pl.multiple_of(lax.rem(oc, per_in) * OUT_COLS + h * half, half)
            x_own = x_all[oc // per_in, pl.ds(pl.multiple_of(me * tokens, tokens), tokens), pl.ds(at, half)]
            val = total[oc, chip, h] + fin_recv[oc, 0, h] + fin_recv[oc, 1, h]
            to = pl.multiple_of(oc * OUT_COLS + h * half, half)
            out_ref[:, pl.ds(to, half)] = (x_own.astype(F32) + val).astype(BF16)

    def down_one(oc, e, obuf):
        val = jnp.dot(hid[e], wout_buf[lax.rem(oc, OUT_DEPTH), e], preferred_element_type=F32)
        obuf[e * capacity:(e + 1) * capacity, :] = val.astype(BF16)

    def down(oc, obuf):
        for e in range(local_e):
            down_one(oc, e, obuf)

    def refill(oc):
        for e in range(local_e):
            wout_copy(e, oc).start()

    def part_sent(oc):
        sent = part_send.at[lax.rem(oc, 2)]
        rcopy(PART, oc, sent, sent, buddy).wait_send()

    def part_rest(oc):
        for t in (c_right, c_left, chip):
            rcopy(PART_REST, oc, part_send.at[lax.rem(oc, 2), t], part_recv.at[oc, t], buddy).start()

    def far_rows(oc, now):
        partial_of(other, c_far, now, part_send.at[lax.rem(oc, 2)])
        partial_of(core, c_far, now, total.at[oc])

    def step(oc, now, nxt, first=False):
        near = (c_right, c_left, chip)
        slot = lax.rem(oc, 2)
        if not first:
            @pl.when(oc >= 2)
            def _():
                part_sent(oc - 2)

        with jax.named_scope("partF"):
            if not first:
                alone(lambda: far_rows(oc, now))
            r_copy(PART, oc).start()
        with jax.named_scope("partA"):
            @alone
            def _():
                for t in near:
                    partial_of(other, t, now, part_send.at[slot])
            part_rest(oc)
        with jax.named_scope("part_wait"):
            r_copy(PART, oc).wait_recv()
        total[oc, c_far] = total[oc, c_far] + part_recv[oc, c_far]
        for kind in (FAR_R, FAR_L):
            r_copy(kind, oc).start()
        if not first:
            with jax.named_scope("far"):
                finish_far(oc - 1)
        if nxt is not None:
            wout_wait(oc + 1)
        with jax.named_scope("partB"):
            @alone
            def _():
                for t in near:
                    partial_of(core, t, now, total.at[oc])
                if nxt is not None:
                    down(oc + 1, nxt)
        with jax.named_scope("rest_wait"):
            rest = part_recv.at[oc, pl.ds(0, chips - 1)]
            rcopy(PART_REST, oc, rest, rest, buddy).wait_recv()
        for t in near:
            total[oc, t] = total[oc, t] + part_recv[oc, t]
        for kind in (NEAR_R, NEAR_L):
            r_copy(kind, oc).start()
        if nxt is not None:
            @pl.when(oc + 1 + OUT_DEPTH < oc_n)
            def _():
                refill(oc + 1 + OUT_DEPTH)
        if not first:
            @pl.when(oc >= LAG)
            def _():
                with jax.named_scope("fin"):
                    finish(oc - LAG)

    with jax.named_scope("up_last"):
        win_wait(last)
        wout_wait(0)

        @alone
        def _():
            gather(last)
            for e in range(local_e):
                up = acc[e] + jnp.dot(xg[e], win_buf[last % IN_DEPTH, e], preferred_element_type=F32)
                hid[e] = gelu(up).astype(BF16)
                if e >= BEHIND:
                    down_one(0, e - BEHIND, obuf0)
            for e in range(local_e - BEHIND, local_e):
                down_one(0, e, obuf0)
            far_rows(0, obuf0)

        refill(OUT_DEPTH)

    step(0, obuf0, obuf1, True)

    @pl.loop(0, oc_n // 2 - 1)
    def _(i):
        step(2 * i + 1, obuf1, obuf0)
        step(2 * i + 2, obuf0, obuf1)

    step(oc_n - 1, obuf1, None)

    d_flush()
    for c in meta_all():
        c.wait_send()

    with jax.named_scope("far_t"):
        finish_far(oc_n - 1)
    for oc in range(oc_n - LAG, oc_n):
        with jax.named_scope("fin_t"):
            finish(oc)

    with jax.named_scope("drain"):
        part_sent(oc_n - 2)
        part_sent(oc_n - 1)
        sent = total.at[:, pl.ds(0, 3)]
        rcopy(FAR_R, 0, sent, sent, buddy).wait_send()


def solution(mesh):
    n = mesh.shape[AXIS]
    row_spec = P(("data", AXIS), None)
    weight_spec = P(AXIS, None, None)

    def device_step(token_rows, expert_ids, gate_weights, w_in, w_out):
        tokens, top_k = expert_ids.shape
        local_e, model, hidden = w_in.shape
        capacity = n * tokens * top_k // (n * local_e)
        slots = local_e * capacity
        chips = n // 2
        kc_n = model // IN_BLOCKS
        oc_n = model // OUT_COLS
        half = OUT_COLS // 2
        hbm = pl.BlockSpec(memory_space=pl.ANY)
        dma = pltpu.SemaphoreType.DMA
        return pl.pallas_call(
            functools.partial(body, n, capacity),
            out_shape=pltpu.VMEM((tokens, model), BF16),
            in_specs=[hbm, hbm, hbm, hbm, hbm],
            out_specs=pl.BlockSpec(memory_space=pltpu.VMEM),
            scratch_shapes=[
                pltpu.VMEM((n, top_k, tokens), jnp.int32),
                pltpu.VMEM((n, top_k, tokens), F32),
                pltpu.VMEM((IN_BLOCKS, n * tokens, kc_n), BF16),
                pltpu.VMEM((n * tokens // PICK_COLS, slots, PICK_COLS), BF16),
                pltpu.VMEM((n, 4 * local_e, tokens), F32),
                pltpu.VMEM((3, n * tokens, slots), BF16),
                pltpu.VMEM((local_e, capacity, kc_n), BF16),
                pltpu.VMEM((local_e, capacity, hidden), F32),
                pltpu.VMEM((local_e, capacity, hidden), BF16),
                pltpu.VMEM((LANES, 4 * slots), BF16),
                pltpu.VMEM((slots, OUT_COLS), BF16),
                pltpu.VMEM((slots, OUT_COLS), BF16),
                pltpu.VMEM((2, chips, 2, tokens, half), F32),
                pltpu.VMEM((oc_n, chips, 2, tokens, half), F32),
                pltpu.VMEM((oc_n, chips, 2, tokens, half), F32),
                pltpu.VMEM((oc_n, 2, tokens, half), F32),
                pltpu.VMEM((oc_n, 2, 2, tokens, half), F32),
                pltpu.VMEM((IN_DEPTH, local_e, kc_n, hidden), BF16),
                pltpu.VMEM((OUT_DEPTH, local_e, hidden, OUT_COLS), BF16),
                dma((2,)), dma((2,)),
                dma, dma((3, IN_BLOCKS)),
                dma((3,)), dma((2, oc_n)), dma((2, 2)),
                dma,
                dma((IN_DEPTH,)),
                dma((OUT_DEPTH,)),
                dma((2,)),
            ],
            compiler_params=pltpu.CompilerParams(
                collective_id=0, has_side_effects=True, vmem_limit_bytes=VMEM_BYTES),
        )(expert_ids.T, gate_weights.T, token_rows, w_in, w_out)

    return jax.shard_map(device_step, mesh=mesh, in_specs=(row_spec, row_spec, row_spec, weight_spec, weight_spec),
                         out_specs=row_spec, check_vma=False)
```

profile of v0, /device:TPU:112, one launch (start us, length us, event | category | flops | bytes accessed | tf_op | source)
XLA Modules:
  0.0 69.7 jit_solution(16873412627709915118)
XLA Ops:
  0.0 68.9 %shard_map.55 = bf16[128,2048]{1,0:T(8,128)(2,1)S(1)} custom-call(s32[6,128]{1,0:T(8,128)} %bitcast.2, f32[6,128]{1,0:T(8,128)} %bitcast.3, bf16[128,2048]{1,0:T(8,128)(2,1)} %x_hbm.1, bf16[8,2048,1408]{2,1,0:T(8,128)(2,1)} %w_in.1, bf16[8,1408,2048]{2,1,0:T(8,128)(2,1)} %w_out.1), custom_call_target="tpu_custom_call" | custom-call | tf_op jit(solution)/shard_map/pallas_call | solution.py:530
  68.9 0.8 %copy.7 = bf16[128,2048]{1,0:T(8,128)(2,1)} copy(bf16[128,2048]{1,0:T(8,128)(2,1)S(1)} %shard_map.55) | data formatting | bytes 1048576
where the time goes:
time: 69.7 us
  Pallas kernels  68.9 us (99%)
  local copies, waits for them, and re-layouts  0.8 us (1%)
    pallas_call x1, Pallas kernels, device_step(): pl.pallas_call(functools.partial(body, n, capacity), out_shape=pltpu.VMEM...  68.9 us

commit v1 on v0

--- a/solution.py
+++ b/solution.py
@@ -203,6 +203,13 @@
         pltpu.make_async_copy(mine, mine, x_sem).wait()
         for kc in range(AHEAD):
             send_own(kc)
+
+    acc[...] = jnp.zeros_like(acc)
+    for q in range(4):
+        at = lax.broadcasted_iota(jnp.int32, (LANES, slots), 1)
+        row = lax.broadcasted_iota(jnp.int32, (LANES, slots), 0) - q * local_e
+        spread[:, q * slots:(q + 1) * slots] = jnp.where(
+            (at >= row * capacity) & (at < (row + 1) * capacity) & (row >= 0) & (row < local_e), 1.0, 0.0).astype(BF16)
 
     with jax.named_scope("meta_wait"):
         for c in meta_all():
@@ -244,15 +251,7 @@
             pick[b * tokens // PICK_COLS, e * capacity:(e + 1) * capacity, at:at + tokens] = jnp.where(
                 slot[e:e + 1, :] == slot_row, 1.0, 0.0).astype(BF16)
 
-    acc[...] = jnp.zeros_like(acc)
-
     part_c = 2 * LANES
-    for q in range(4):
-        at = lax.broadcasted_iota(jnp.int32, (LANES, slots), 1)
-        row = lax.broadcasted_iota(jnp.int32, (LANES, slots), 0) - q * local_e
-        spread[:, q * slots:(q + 1) * slots] = jnp.where(
-            (at >= row * capacity) & (at < (row + 1) * capacity) & (row >= 0) & (row < local_e), 1.0, 0.0).astype(BF16)
-
     def mix_rows(b):
         row = pl.multiple_of((lax.rem(b, 2) * chips + b // 2) * tokens, tokens)
         cols = jnp.concatenate(
@@ -427,6 +426,8 @@
             if not first:
                 alone(lambda: far_rows(oc, now))
             r_copy(PART, oc).start()
+            if first:
+                refill(OUT_DEPTH)
         with jax.named_scope("partA"):
             @alone
             def _():
@@ -482,8 +483,6 @@
             for e in range(local_e - BEHIND, local_e):
                 down_one(0, e, obuf0)
             far_rows(0, obuf0)
-
-        refill(OUT_DEPTH)
 
     step(0, obuf0, obuf1, True)
 

time: 69.7 us -> 69.7 us (level)
  no operation moved by 1% of the time
where the time goes in v1:
time: 69.7 us
  Pallas kernels  68.9 us (99%)
  local copies, waits for them, and re-layouts  0.8 us (1%)
    pallas_call x1, Pallas kernels, device_step(): pl.pallas_call(functools.partial(body, n, capacity), out_shape=pltpu.VMEM...  68.9 us

profile of v1, /device:TPU:112, one launch (start us, length us, event | category | flops | bytes accessed | tf_op | source)
XLA Modules:
  0.0 69.7 jit_solution(4750386226360987051)
XLA Ops:
  0.0 68.9 %shard_map.55 = bf16[128,2048]{1,0:T(8,128)(2,1)S(1)} custom-call(s32[6,128]{1,0:T(8,128)} %bitcast.2, f32[6,128]{1,0:T(8,128)} %bitcast.3, bf16[128,2048]{1,0:T(8,128)(2,1)} %x_hbm.1, bf16[8,2048,1408]{2,1,0:T(8,128)(2,1)} %w_in.1, bf16[8,1408,2048]{2,1,0:T(8,128)(2,1)} %w_out.1), custom_call_target="tpu_custom_call" | custom-call | tf_op jit(solution)/shard_map/pallas_call | solution.py:529
  68.9 0.8 %copy.7 = bf16[128,2048]{1,0:T(8,128)(2,1)} copy(bf16[128,2048]{1,0:T(8,128)(2,1)S(1)} %shard_map.55) | data formatting | bytes 1048576
